TPU v7x, 32 devices: a whole 2x2x4 slice. The times are simulated.
32 devices in a mesh: dp: 8 (over z, y), mp: 4 (over x, core).
Axes of the slice: x: 2, y: 2, z: 4, core: 2. Of those that a mesh axis runs over, the one named last changes fastest.
Arguments:
- prefix_hidden: bfloat16 [32, 1024, 2048], P(('dp', 'mp')), may hold values from -6 to 6
- prefix_len: int32 [32], P('dp'), may hold values from 256 to 1024
- actions: float32 [32, 50, 32], P('dp'), may hold values from -6 to 6
- noise: float32 [32, 50, 32], P('dp'), may hold values from -6 to 6
- time_index: int32 [32], P('dp'), may hold values from 0 to 999
- prefix_gain: float32 [2048], replicated, may hold values from 0.25 to 1.75
- key_weight: bfloat16 [2048, 256], P('dp'), may hold values from -0.125 to 0.125
- value_weight: bfloat16 [2048, 256], P('dp'), may hold values from -0.125 to 0.125
- action_in: bfloat16 [32, 1024], replicated, may hold values from -1 to 1
- attn_gain: float32 [1024], replicated, may hold values from 0.25 to 1.75
- query_w: bfloat16 [1024, 2048], P('dp', 'mp'), may hold values from -0.1875 to 0.1875
- akey_w: bfloat16 [1024, 256], P('dp'), may hold values from -0.1875 to 0.1875
- avalue_w: bfloat16 [1024, 256], P('dp'), may hold values from -0.1875 to 0.1875
- out_w: bfloat16 [2048, 1024], P('mp', 'dp'), may hold values from -0.125 to 0.125
- mlp_gain: float32 [1024], replicated, may hold values from 0.25 to 1.75
- gate_w: bfloat16 [1024, 4096], P('dp', 'mp'), may hold values from -0.1875 to 0.1875
- up_w: bfloat16 [1024, 4096], P('dp', 'mp'), may hold values from -0.1875 to 0.1875
- down_w: bfloat16 [4096, 1024], P('mp', 'dp'), may hold values from -0.09375 to 0.09375
- final_gain: float32 [1024], replicated, may hold values from 0.25 to 1.75
- head_w: bfloat16 [1024, 32], replicated, may hold values from -0.1875 to 0.1875
Outputs:
- velocity: float32 [32, 50, 32], P(('dp', 'mp'))
- ep_loss: float32 [32], P(('dp', 'mp'))
Inputs may be any that keep to these rules, and one draw needn't show every extreme that they name: `prefix_len`: prefix positions at or above an episode's length are padding that no output reads.
All inputs are finite; a program needn't handle non-finite values.
Results may differ from a plain program's by a relative error of at most 0.009.
Values may be sent and summed in bfloat16 or wider, within the bound.
No kernel may reach another device: no remote copies, remote signals or barrier semaphores. Data moves between devices by JAX's collectives and lax.ppermute only.
A program may use at most 64 MiB of HBM per device.

v0:
```python
import math
import jax
import jax.numpy as jnp
from jax import lax
from jax.sharding import PartitionSpec as P

TSTEPS = 1000


def rms(values, gain):
    return values * lax.rsqrt(jnp.mean(values * values, axis=-1, keepdims=True) + 1e-06) * gain


def time_embed(times, width):
    half = width // 2
    steps = jnp.arange(half, dtype=jnp.float32)
    period = 0.004 * jnp.power(jnp.float32(1000.0), steps / (half - 1))
    angle = times[:, None] * (2.0 * math.pi) / period[None, :]
    return jnp.concatenate([jnp.sin(angle), jnp.cos(angle)], axis=-1)


def attend(query, pkeys, pvals, akeys, avals, lengths):
    live = jnp.arange(pkeys.shape[1], dtype=jnp.int32)[None, :] < lengths[:, None]
    scores = jnp.einsum("erd,epd->erp", query, pkeys, preferred_element_type=jnp.float32)
    probs = jnp.where(live[:, None, :], jnp.exp(scores), 0.0)
    action_scores = jnp.einsum("erd,ecd->erc", query, akeys, preferred_element_type=jnp.float32)
    action_probs = jnp.exp(action_scores)
    denom = jnp.sum(probs, axis=-1) + jnp.sum(action_probs, axis=-1)
    weighted = jnp.einsum(
        "erp,epd->erd", probs.astype(jnp.bfloat16), pvals, preferred_element_type=jnp.float32
    )
    weighted = weighted + jnp.einsum(
        "erc,ecd->erd", action_probs.astype(jnp.bfloat16), avals, preferred_element_type=jnp.float32
    )
    return (weighted / denom[:, :, None]).astype(jnp.bfloat16)


def on_device(
    prefix_hidden,
    prefix_len,
    actions,
    noise,
    time_index,
    prefix_gain,
    key_weight,
    value_weight,
    action_in,
    attn_gain,
    query_w,
    akey_w,
    avalue_w,
    out_w,
    mlp_gain,
    gate_w,
    up_w,
    down_w,
    final_gain,
    head_w,
):
    own_eps, positions, width = prefix_hidden.shape
    group_eps, span, adim = actions.shape
    expert = action_in.shape[1]
    head_size = key_weight.shape[1]
    local_heads = query_w.shape[1] // head_size
    rows_total = group_eps * span
    own_rows = own_eps * span
    member = lax.axis_index("mp")
    first_row = member * own_rows
    first_ep = member * own_eps
    times = (time_index.astype(jnp.float32) + 0.5) / TSTEPS
    x_t = times[:, None, None] * noise + (1.0 - times)[:, None, None] * actions
    target = noise - actions
    x_in = x_t.reshape(rows_total, adim).astype(jnp.bfloat16)
    temb = time_embed(times, expert)
    h0 = (
        jnp.dot(x_in, action_in, preferred_element_type=jnp.float32).reshape(
            group_eps, span, expert
        )
        + temb[:, None, :]
    )
    h0 = h0.reshape(rows_total, expert)
    key_full, value_full = (
        lax.all_gather(key_weight, "dp", axis=0, tiled=True),
        lax.all_gather(value_weight, "dp", axis=0, tiled=True),
    )
    prefix_normed = rms(
        prefix_hidden.reshape(own_eps * positions, width).astype(jnp.float32), prefix_gain
    ).astype(jnp.bfloat16)
    pkeys = (
        jnp.dot(prefix_normed, key_full, preferred_element_type=jnp.float32)
        .astype(jnp.bfloat16)
        .reshape(own_eps, positions, head_size)
    )
    pvals = (
        jnp.dot(prefix_normed, value_full, preferred_element_type=jnp.float32)
        .astype(jnp.bfloat16)
        .reshape(own_eps, positions, head_size)
    )
    normed = rms(h0, attn_gain).astype(jnp.bfloat16)
    query_full, akey_full, avalue_full = (
        lax.all_gather(query_w, "dp", axis=0, tiled=True),
        lax.all_gather(akey_w, "dp", axis=0, tiled=True),
        lax.all_gather(avalue_w, "dp", axis=0, tiled=True),
    )
    query = (
        jnp.dot(normed, query_full, preferred_element_type=jnp.float32) * head_size ** (-0.5)
    ).astype(jnp.bfloat16)
    akeys = (
        jnp.dot(normed, akey_full, preferred_element_type=jnp.float32)
        .astype(jnp.bfloat16)
        .reshape(group_eps, span, head_size)
    )
    avals = (
        jnp.dot(normed, avalue_full, preferred_element_type=jnp.float32)
        .astype(jnp.bfloat16)
        .reshape(group_eps, span, head_size)
    )
    keys_all, vals_all = (
        lax.all_gather(pkeys, "mp", axis=0, tiled=True),
        lax.all_gather(pvals, "mp", axis=0, tiled=True),
    )
    attn = attend(
        query.reshape(group_eps, span * local_heads, head_size),
        keys_all,
        vals_all,
        akeys,
        avals,
        prefix_len,
    )
    attn = attn.reshape(rows_total, local_heads * head_size)
    out_full = lax.all_gather(out_w, "dp", axis=1, tiled=True)
    gate_full, up_full = (
        lax.all_gather(gate_w, "dp", axis=0, tiled=True),
        lax.all_gather(up_w, "dp", axis=0, tiled=True),
    )
    down_full = lax.all_gather(down_w, "dp", axis=1, tiled=True)
    h0_own = lax.dynamic_slice_in_dim(h0, first_row, own_rows, 0)
    h1 = h0_own + lax.psum_scatter(
        jnp.dot(attn, out_full, preferred_element_type=jnp.float32).astype(jnp.bfloat16),
        "mp",
        scatter_dimension=0,
        tiled=True,
    ).astype(jnp.float32)
    mixed_own = rms(h1, mlp_gain).astype(jnp.bfloat16)
    mixed = lax.all_gather(mixed_own, "mp", axis=0, tiled=True)
    gate = jnp.dot(mixed, gate_full, preferred_element_type=jnp.float32)
    upper = jnp.dot(mixed, up_full, preferred_element_type=jnp.float32)
    hidden = (jax.nn.gelu(gate, approximate=True) * upper).astype(jnp.bfloat16)
    h2 = h1 + lax.psum_scatter(
        jnp.dot(hidden, down_full, preferred_element_type=jnp.float32).astype(jnp.bfloat16),
        "mp",
        scatter_dimension=0,
        tiled=True,
    ).astype(jnp.float32)
    final = rms(h2, final_gain).astype(jnp.bfloat16)
    velocity = jnp.dot(final, head_w, preferred_element_type=jnp.float32).reshape(
        own_eps, span, adim
    )
    own_target = lax.dynamic_slice_in_dim(target, first_ep, own_eps, 0)
    diff = velocity - own_target
    ep_loss = jnp.mean(diff * diff, axis=(1, 2))
    return (velocity, ep_loss)


def solution(mesh):
    in_specs = (
        P(("dp", "mp"), None, None),
        P("dp"),
        P("dp", None, None),
        P("dp", None, None),
        P("dp"),
        P(),
        P("dp", None),
        P("dp", None),
        P(),
        P(),
        P("dp", "mp"),
        P("dp", None),
        P("dp", None),
        P("mp", "dp"),
        P(),
        P("dp", "mp"),
        P("dp", "mp"),
        P("mp", "dp"),
        P(),
        P(),
    )
    out_specs = (P(("dp", "mp"), None, None), P(("dp", "mp")))
    return jax.shard_map(
        on_device, mesh=mesh, in_specs=in_specs, out_specs=out_specs, check_vma=False
    )
```

profile of v0, /device:TPU:6, one launch (start us, length us, event | category | flops | bytes accessed | tf_op | source)
XLA Modules:
  0.0 404.9 jit_solution(4263375516487390356)
XLA Ops:
  7.2 0.0 all-gather.15.cloned.1.call-start
  7.2 0.7 all-gather.15.cloned.1.call-update
  7.9 0.0 all-gather.17.cloned.1.call-start
  8.0 0.7 all-gather.17.cloned.1.call-update
  8.7 0.0 all-gather.13.cloned.1.call-start
  8.7 0.7 all-gather.13.cloned.1.call-update
  9.4 0.0 all-gather.27.cloned.1.call-start
  9.5 3.1 fusion.2
  12.5 38.1 %all-gather.15.cloned.1.call-done = bf16[2048,256]{1,0:T(8,128)(2,1)} async-done(((bf16[256,256]{1,0:T(8,128)(2,1)}), bf16[2048,256]{1,0:T(8,128)(2,1)}) %all-gather.15.cloned.1.call-update) | async-done | bytes 1048592 | tf_op jit(solution)/shard_map/all_gather | solution.py:83
  50.7 4.6 %convolution_convert_fusion.1 = bf16[1024,256]{1,0:T(8,128)(2,1)} fusion(bf16[2048,256]{1,0:T(8,128)(2,1)} %all-gather.15.cloned.1.call-done, bf16[1,1024,2048]{2,1,0:T(8,128)(2,1)} %param.20, f32[2048]{0:T(1024)S(1)} %copy-done.12, f32[1024]{0:T(1024)S(1)} %add_rsqrt_fusion), kind=kOutput, calls=%fused_computation.9 | convolution fusion | flops 1082392576 | bytes 5779456 | tf_op jit(solution)/shard_map/dot_general | solution.py:90
  55.3 0.0 all-gather.27.cloned.1.call-update
  55.4 0.0 all-gather.29.cloned.1.call-start
  55.4 36.4 %all-gather.17.cloned.1.call-done = bf16[2048,256]{1,0:T(8,128)(2,1)} async-done(((bf16[256,256]{1,0:T(8,128)(2,1)}), bf16[2048,256]{1,0:T(8,128)(2,1)}) %all-gather.17.cloned.1.call-update) | async-done | bytes 1048592 | tf_op jit(solution)/shard_map/all_gather | solution.py:84
  91.8 4.6 %convolution_convert_fusion = bf16[1024,256]{1,0:T(8,128)(2,1)} fusion(bf16[2048,256]{1,0:T(8,128)(2,1)} %all-gather.17.cloned.1.call-done, bf16[1,1024,2048]{2,1,0:T(8,128)(2,1)} %param.20, f32[2048]{0:T(1024)S(1)} %copy-done.12, f32[1024]{0:T(1024)S(1)} %add_rsqrt_fusion), kind=kOutput, calls=%fused_computation.8 | convolution fusion | flops 1082392576 | bytes 5779456 | tf_op jit(solution)/shard_map/dot_general | solution.py:95
  96.4 0.0 all-gather.29.cloned.1.call-update
  96.5 0.0 all-gather.19.cloned.1.call-start
  96.5 0.5 all-gather.19.cloned.1.call-update
  97.0 0.0 all-gather.21.cloned.1.call-start
  97.1 0.7 all-gather.21.cloned.1.call-update
  97.8 0.0 all-gather.23.cloned.1.call-start
  97.8 0.7 all-gather.23.cloned.1.call-update
  98.5 0.0 all-gather.25.cloned.1.call-start
  98.6 0.7 all-gather.25.cloned.1.call-update
  99.3 0.1 fusion.38
  99.5 0.5 multiply_reduce_fusion
  100.0 0.1 reshape.115
  100.1 0.1 rsqrt.36
  100.2 30.9 %all_gather.41 = bf16[1024,256]{1,0:T(8,128)(2,1)S(1)} all-gather(bf16[128,256]{1,0:T(8,128)(2,1)S(1)} %copy-done.3), channel_id=1, replica_groups=mesh['dp'=8,'mp'=4] {'dp'}, dimensions={0}, use_global_device_ids=true | all-gather | bytes 589824 | tf_op jit(solution)/shard_map/all_gather | solution.py:102
  131.1 0.1 multiply_convert_fusion
  131.2 0.3 convolution_convert_fusion.5
  131.6 31.5 %all_gather.42 = bf16[1024,256]{1,0:T(8,128)(2,1)S(1)} all-gather(bf16[128,256]{1,0:T(8,128)(2,1)S(1)} %copy-done.4), channel_id=1, replica_groups=mesh['dp'=8,'mp'=4] {'dp'}, dimensions={0}, use_global_device_ids=true | all-gather | bytes 589824 | tf_op jit(solution)/shard_map/all_gather | solution.py:103
  163.1 0.3 convolution_convert_fusion.4
  163.5 0.1 iota_compare_fusion
  163.5 1.6 fusion.10
  165.1 0.1 reshape.116
  165.2 0.2 fusion.46
  165.5 0.0 all-gather.27.cloned.1.call-done
  165.5 2.5 fusion.45
  168.0 14.4 %all-gather.29.cloned.1.call-done = bf16[4096,256]{1,0:T(8,128)(2,1)} async-done(((bf16[1024,256]{1,0:T(8,128)(2,1)}), bf16[4096,256]{1,0:T(8,128)(2,1)}) %all-gather.29.cloned.1.call-update) | async-done | bytes 2097168 | tf_op jit(solution)/shard_map/all_gather | solution.py:120
  182.4 2.0 fusion.11
  184.5 0.3 fusion.9
  184.7 0.1 reshape.121
  184.8 39.4 %all-gather.19.cloned.1.call-done = bf16[512,1024]{1,0:T(8,128)(2,1)} async-done(((bf16[512,128]{1,0:T(8,128)(2,1)}), bf16[512,1024]{1,0:T(8,128)(2,1)}) %all-gather.19.cloned.1.call-update) | async-done | bytes 1048592 | tf_op jit(solution)/shard_map/all_gather | solution.py:131
  224.2 1.6 convolution_convert_fusion.3
  225.8 10.1 %fusion = bf16[56,1024]{1,0:T(8,128)(2,1)S(1)} fusion(bf16[200,1024]{1,0:T(8,128)(2,1)S(1)} %convolution_convert_fusion.3), kind=kCustom, calls=%all-reduce-scatter | all-reduce-scatter fusion | flops 229377 | bytes 524800
  236.0 1.9 collective-permute-start
  237.9 0.6 dynamic-slice.6
  239.1 2.2 collective-permute-done
  241.4 0.2 concatenate.4
  241.6 0.2 multiply_reduce_fusion.2
  241.8 0.1 fusion.25
  241.9 6.3 %all-gather.2 = bf16[4,50,1024]{2,1,0:T(8,128)(2,1)S(1)} all-gather(bf16[1,50,1024]{2,1,0:T(8,128)(2,1)S(1)} %fusion.25), channel_id=1, replica_groups=mesh['dp'=8,'mp'=4] {'mp'}, dimensions={0}, use_global_device_ids=true | all-gather | bytes 512000 | tf_op jit(solution)/shard_map/all_gather | solution.py:145
  248.2 0.1 reshape.127
  248.3 25.8 %all-gather.21.cloned.1.call-done = bf16[1024,1024]{1,0:T(8,128)(2,1)} async-done(((bf16[128,1024]{1,0:T(8,128)(2,1)}), bf16[1024,1024]{1,0:T(8,128)(2,1)}) %all-gather.21.cloned.1.call-update) | async-done | bytes 2097168 | tf_op jit(solution)/shard_map/all_gather | solution.py:133
  274.1 2.2 fusion.47
  276.3 47.6 %all-gather.23.cloned.1.call-done = bf16[1024,1024]{1,0:T(8,128)(2,1)} async-done(((bf16[128,1024]{1,0:T(8,128)(2,1)}), bf16[1024,1024]{1,0:T(8,128)(2,1)}) %all-gather.23.cloned.1.call-update) | async-done | bytes 2097168 | tf_op jit(solution)/shard_map/all_gather | solution.py:134
  323.8 51.9 %all-gather.25.cloned.1.call-done = bf16[1024,1024]{1,0:T(8,128)(2,1)} async-done(((bf16[1024,128]{1,0:T(8,128)(2,1)}), bf16[1024,1024]{1,0:T(8,128)(2,1)}) %all-gather.25.cloned.1.call-update) | async-done | bytes 2097168 | tf_op jit(solution)/shard_map/all_gather | solution.py:136
  375.7 3.3 convolution_convert_fusion.2
  379.0 10.2 %fusion.1 = bf16[56,1024]{1,0:T(8,128)(2,1)S(1)} fusion(bf16[200,1024]{1,0:T(8,128)(2,1)S(1)} %convolution_convert_fusion.2), kind=kCustom, calls=%all-reduce-scatter.1 | all-reduce-scatter fusion | flops 229377 | bytes 524800
  389.3 1.9 collective-permute-start.1
  391.2 3.5 collective-permute-done.1
  394.7 0.2 concatenate.5
  394.9 0.2 multiply_reduce_fusion.1
  395.1 1.5 fusion.35
  (39 shorter events, 0.2 us)
Async XLA Ops:
  7.2 92.3 %copy-start = (bf16[32,1024]{1,0:T(8,128)(2,1)S(1)}, bf16[32,1024]{1,0:T(8,128)(2,1)}, u32[]{:S(2)}) copy-start(bf16[32,1024]{1,0:T(8,128)(2,1)} %param.28) | copy-start | bytes 196612
  7.2 43.5 %all-gather.15.cloned.1.call-start = ((), (), s32[]{:S(2)}) async-start(), calls=%async_computation.1 | async-start | bytes 1179648 | tf_op jit(solution)/shard_map/all_gather | solution.py:83
  7.9 83.9 %all-gather.17.cloned.1.call-start = ((), (), s32[]{:S(2)}) async-start(), calls=%async_computation.2 | async-start | bytes 1179648 | tf_op jit(solution)/shard_map/all_gather | solution.py:84
  8.7 154.9 %all-gather.13.cloned.1.call-start = ((), (), s32[]{:S(2)}) async-start(), calls=%async_computation | async-start | bytes 1179648 | tf_op jit(solution)/shard_map/all_gather | solution.py:101
  9.4 41.3 %copy-start.12 = (f32[2048]{0:T(1024)S(1)}, f32[2048]{0:T(1024)}, u32[]{:S(2)}) copy-start(f32[2048]{0:T(1024)} %param.25) | copy-start | bytes 24580
  9.4 156.1 %all-gather.27.cloned.1.call-start = ((), (), s32[]{:S(2)}) async-start(), calls=%async_computation.7 | async-start | bytes 2621440 | tf_op jit(solution)/shard_map/all_gather | solution.py:119
  55.4 43.9 %copy-start.11 = (s32[4]{0:T(128)S(1)}, s32[4]{0:T(128)}, u32[]{:S(2)}) copy-start(s32[4]{0:T(128)} %param.24) | copy-start | bytes 52
  55.4 44.1 %copy-start.1 = (f32[4,50,32]{1,2,0:T(8,128)S(1)}, f32[4,50,32]{1,2,0:T(8,128)}, u32[]{:S(2)}) copy-start(f32[4,50,32]{1,2,0:T(8,128)} %param.22) | copy-start | bytes 76804
  55.4 44.1 %copy-start.2 = (f32[4,50,32]{1,2,0:T(8,128)S(1)}, f32[4,50,32]{1,2,0:T(8,128)}, u32[]{:S(2)}) copy-start(f32[4,50,32]{1,2,0:T(8,128)} %param.23) | copy-start | bytes 76804
  55.4 127.0 %all-gather.29.cloned.1.call-start = ((), (), s32[]{:S(2)}) async-start(), calls=%async_computation.8 | async-start | bytes 2621440 | tf_op jit(solution)/shard_map/all_gather | solution.py:120
  96.4 3.8 copy-start.3
  96.5 127.8 %all-gather.19.cloned.1.call-start = ((), (), s32[]{:S(2)}) async-start(), calls=%async_computation.3 | async-start | bytes 1179648 | tf_op jit(solution)/shard_map/all_gather | solution.py:131
  97.0 34.1 %copy-start.6 = (f32[1024]{0:T(1024)S(1)}, f32[1024]{0:T(1024)}, u32[]{:S(2)}) copy-start(f32[1024]{0:T(1024)} %param.29) | copy-start | bytes 12292
  97.0 177.0 %all-gather.21.cloned.1.call-start = ((), (), s32[]{:S(2)}) async-start(), calls=%async_computation.4 | async-start | bytes 2359296 | tf_op jit(solution)/shard_map/all_gather | solution.py:133
  97.8 226.0 %all-gather.23.cloned.1.call-start = ((), (), s32[]{:S(2)}) async-start(), calls=%async_computation.5 | async-start | bytes 2359296 | tf_op jit(solution)/shard_map/all_gather | solution.py:134
  98.5 277.1 %all-gather.25.cloned.1.call-start = ((), (), s32[]{:S(2)}) async-start(), calls=%async_computation.6 | async-start | bytes 2359296 | tf_op jit(solution)/shard_map/all_gather | solution.py:136
  100.0 31.6 %copy-start.4 = (bf16[128,256]{1,0:T(8,128)(2,1)S(1)}, bf16[128,256]{1,0:T(8,128)(2,1)}, u32[]{:S(2)}) copy-start(bf16[128,256]{1,0:T(8,128)(2,1)} %param.32) | copy-start | bytes 196612
  131.1 32.4 %copy-start.9 = (s32[4]{0:T(128)S(1)}, s32[4]{0:T(128)}, u32[]{:S(2)}) copy-start(s32[4]{0:T(128)} %param.21) | copy-start | bytes 52
  184.5 53.4 %copy-start.10 = (u32[32]{0:T(128)S(1)}, u32[32]{0:T(128)}, u32[]{:S(2)}) copy-start(u32[32]{0:T(128)} %constant.63) | copy-start | bytes 388
  184.7 57.0 %copy-start.7 = (f32[1024]{0:T(1024)S(1)}, f32[1024]{0:T(1024)}, u32[]{:S(2)}) copy-start(f32[1024]{0:T(1024)} %param.34) | copy-start | bytes 12292
  236.0 5.4 %collective-permute-start = (bf16[18,1024]{1,0:T(8,128)(2,1)S(1)}, bf16[18,1024]{1,0:T(8,128)(2,1)S(1)}, u32[]{:S(2)}, u32[]{:S(2)}) collective-permute-start(bf16[18,1024]{1,0:T(8,128)(2,1)S(1)} %slice), channel_id=1, source_target_pairs={{0,1},{1,2},{2,3},{4,5},{5,6},{6,7},{8,9},{9,10},{10,11},{12,13},{... | collective-permute-start | bytes 110600
  276.2 118.9 %copy-start.5 = (bf16[1024,32]{0,1:T(8,128)(2,1)S(1)}, bf16[1024,32]{0,1:T(8,128)(2,1)}, u32[]{:S(2)}) copy-start(bf16[1024,32]{0,1:T(8,128)(2,1)} %param.39) | copy-start | bytes 196612
  276.3 118.9 %copy-start.8 = (f32[1024]{0:T(1024)S(1)}, f32[1024]{0:T(1024)}, u32[]{:S(2)}) copy-start(f32[1024]{0:T(1024)} %param.38) | copy-start | bytes 12292
  389.3 5.4 %collective-permute-start.1 = (bf16[18,1024]{1,0:T(8,128)(2,1)S(1)}, bf16[18,1024]{1,0:T(8,128)(2,1)S(1)}, u32[]{:S(2)}, u32[]{:S(2)}) collective-permute-start(bf16[18,1024]{1,0:T(8,128)(2,1)S(1)} %slice.1), channel_id=1, source_target_pairs={{0,1},{1,2},{2,3},{4,5},{5,6},{6,7},{8,9},{9,10},{10,11},{12,13},{... | collective-permute-start | bytes 110600
Sparse Core Ops, SparseCore 0:
  10.1 40.5 all-gather.14
  52.8 38.9 all-gather.16
  94.0 41.6 all-gather.12
  137.0 21.2 all-gather.26
  159.8 22.5 all-gather.28
  184.3 39.8 all-gather.18
  226.3 47.6 all-gather.20
  276.2 47.6 all-gather.22
  325.9 49.7 all-gather.24
where the time goes:
time: 405 us
  waiting for transfers between devices  264 us (65%)
  blocking collectives  89.1 us (22%)
  matrix products  25.5 us (6%)
  between operations  16.7 us (4%)
  starting transfers between devices  4.19 us (1%)
    all_gather x1, waiting for transfers between devices, on_device(): down_full = lax.all_gather(down_w, 'dp', axis=1, tiled=True)  51.9 us
    all_gather x1, waiting for transfers between devices, on_device(): lax.all_gather(up_w, 'dp', axis=0, tiled=True)  47.6 us
    all_gather x1, waiting for transfers between devices, on_device(): out_full = lax.all_gather(out_w, 'dp', axis=1, tiled=True)  39.4 us
    all_gather x1, waiting for transfers between devices, on_device(): lax.all_gather(key_weight, 'dp', axis=0, tiled=True)  38.1 us
    all_gather x1, waiting for transfers between devices, on_device(): lax.all_gather(value_weight, 'dp', axis=0, tiled=True)  36.4 us
    all_gather x1, blocking collectives, on_device(): lax.all_gather(avalue_w, 'dp', axis=0, tiled=True)  31.5 us
    all_gather x1, blocking collectives, on_device(): lax.all_gather(akey_w, 'dp', axis=0, tiled=True)  30.9 us
    all_gather x1, waiting for transfers between devices, on_device(): lax.all_gather(gate_w, 'dp', axis=0, tiled=True)  25.8 us
  transfers between devices with their start and end apart: 11, of which 9 were waited for; matrix products, arithmetic and copies ran while one was open for 9% of the time, Pallas kernels for 0%

commit v1 on v0

--- a/solution.py
+++ b/solution.py
@@ -133,7 +133,13 @@
         lax.all_gather(gate_w, "dp", axis=0, tiled=True),
         lax.all_gather(up_w, "dp", axis=0, tiled=True),
     )
-    down_full = lax.all_gather(down_w, "dp", axis=1, tiled=True)
+    size = lax.axis_size("dp")
+    block, pieces = (down_w, [down_w])
+    for _ in range(size - 1):
+        block = lax.ppermute(block, "dp", [(i, (i + 1) % size) for i in range(size)])
+        pieces.insert(0, block)
+    line = jnp.concatenate(pieces, axis=1)
+    down_full = jnp.roll(line, (lax.axis_index("dp") + 1) * down_w.shape[1], axis=1)
     h0_own = lax.dynamic_slice_in_dim(h0, first_row, own_rows, 0)
     h1 = h0_own + lax.psum_scatter(
         jnp.dot(attn, out_full, preferred_element_type=jnp.float32).astype(jnp.bfloat16),

time: 405 us -> 361 us (0.89)
  waiting for transfers between devices: 264 us -> 178 us
  starting transfers between devices: 4.19 us -> 22.2 us
  local copies, waits for them, and re-layouts: 1.63 us -> 18.1 us
  blocking collectives: 89.1 us -> 93.4 us
    all_gather x1 -> x0, waiting for transfers between devices: 51.9 us -> none  [on_device(): down_full = lax.all_gather(down_w, 'dp', axis=1, tiled=True)]
    all_gather x1, waiting for transfers between devices: 39.4 us -> 0.02 us  [on_device(): out_full = lax.all_gather(out_w, 'dp', axis=1, tiled=True)]
    ppermute x0 -> x7, waiting for transfers between devices: none -> 27.3 us  [on_device(): lax.ppermute(block, 'dp', [(i, (i + 1) % size) for i in range(size)])]
    ppermute x0 -> x7, starting transfers between devices: none -> 18.1 us  [on_device(): lax.ppermute(block, 'dp', [(i, (i + 1) % size) for i in range(size)])]
    unnamed x32 -> x53, local copies, waits for them, and re-layouts: 1.19 us -> 16.3 us
    all_gather x1, waiting for transfers between devices: 14.4 us -> 0.02 us  [on_device(): lax.all_gather(pvals, 'mp', axis=0, tiled=True)]
    all_gather x1, waiting for transfers between devices: 25.8 us -> 19.5 us  [on_device(): lax.all_gather(gate_w, 'dp', axis=0, tiled=True)]
    unnamed x11 -> x10, waiting for transfers between devices: 10.4 us -> 9.51 us
  transfers between devices with their start and end apart: 11 -> 17, of which waited for: 9 -> 11; matrix products, arithmetic and copies ran while one was open for 9% -> 14% of each run, Pallas kernels for 0% -> 0%
where the time goes in v1:
time: 361 us; the launch traced here: 359 us
  waiting for transfers between devices  178 us (49%)
  blocking collectives  93.4 us (26%)
  matrix products  26.2 us (7%)
  starting transfers between devices  22.2 us (6%)
  local copies, waits for them, and re-layouts  18.1 us (5%)
  between operations  17 us (5%)
  other arithmetic  3.95 us (1%)
    all_gather x1, waiting for transfers between devices, on_device(): lax.all_gather(up_w, 'dp', axis=0, tiled=True)  47.6 us
    all_gather x1, waiting for transfers between devices, on_device(): lax.all_gather(key_weight, 'dp', axis=0, tiled=True)  38.1 us
    all_gather x1, waiting for transfers between devices, on_device(): lax.all_gather(value_weight, 'dp', axis=0, tiled=True)  36.4 us
    all_gather x1, blocking collectives, on_device(): lax.all_gather(akey_w, 'dp', axis=0, tiled=True)  34.3 us
    all_gather x1, blocking collectives, on_device(): lax.all_gather(avalue_w, 'dp', axis=0, tiled=True)  34.1 us
    ppermute x7, waiting for transfers between devices, on_device(): lax.ppermute(block, 'dp', [(i, (i + 1) % size) for i in range(size)])  27.3 us
    all_gather x1, waiting for transfers between devices, on_device(): lax.all_gather(gate_w, 'dp', axis=0, tiled=True)  19.5 us
    unnamed x2, blocking collectives  18.6 us
  transfers between devices with their start and end apart: 17, of which 11 were waited for; matrix products, arithmetic and copies ran while one was open for 14% of the time, Pallas kernels for 0%

profile of v1, /device:TPU:6, one launch (start us, length us, event | category | flops | bytes accessed | tf_op | source)
XLA Modules:
  0.0 359.4 jit_solution(6073681266011720273)
XLA Ops:
  7.2 0.7 all-gather.14.cloned.1.call-update
  8.0 0.7 all-gather.16.cloned.1.call-update
  8.7 0.7 all-gather.12.cloned.1.call-update
  9.5 3.1 fusion.2
  12.5 38.1 %all-gather.14.cloned.1.call-done = bf16[2048,256]{1,0:T(8,128)(2,1)} async-done(((bf16[256,256]{1,0:T(8,128)(2,1)}), bf16[2048,256]{1,0:T(8,128)(2,1)}) %all-gather.14.cloned.1.call-update) | async-done | bytes 1048592 | tf_op jit(solution)/shard_map/all_gather | solution.py:83
  50.7 4.6 %convolution_convert_fusion.1 = bf16[1024,256]{1,0:T(8,128)(2,1)} fusion(bf16[2048,256]{1,0:T(8,128)(2,1)} %all-gather.14.cloned.1.call-done, bf16[1,1024,2048]{2,1,0:T(8,128)(2,1)} %param.20, f32[2048]{0:T(1024)S(1)} %copy-done.15, f32[1024]{0:T(1024)S(1)} %add_rsqrt_fusion), kind=kOutput, calls=%fused_computation.11 | convolution fusion | flops 1082392576 | bytes 5779456 | tf_op jit(solution)/shard_map/dot_general | solution.py:90
  55.4 36.4 %all-gather.16.cloned.1.call-done = bf16[2048,256]{1,0:T(8,128)(2,1)} async-done(((bf16[256,256]{1,0:T(8,128)(2,1)}), bf16[2048,256]{1,0:T(8,128)(2,1)}) %all-gather.16.cloned.1.call-update) | async-done | bytes 1048592 | tf_op jit(solution)/shard_map/all_gather | solution.py:84
  91.8 4.6 %convolution_convert_fusion = bf16[1024,256]{1,0:T(8,128)(2,1)} fusion(bf16[2048,256]{1,0:T(8,128)(2,1)} %all-gather.16.cloned.1.call-done, bf16[1,1024,2048]{2,1,0:T(8,128)(2,1)} %param.20, f32[2048]{0:T(1024)S(1)} %copy-done.15, f32[1024]{0:T(1024)S(1)} %add_rsqrt_fusion), kind=kOutput, calls=%fused_computation.10 | convolution fusion | flops 1082392576 | bytes 5779456 | tf_op jit(solution)/shard_map/dot_general | solution.py:95
  96.5 0.5 all-gather.18.cloned.1.call-update
  97.1 0.7 all-gather.20.cloned.1.call-update
  97.9 1.3 collective-permute-start
  99.2 6.5 %collective-permute-done = bf16[1024,128]{1,0:T(8,128)(2,1)S(1)} collective-permute-done((bf16[1024,128]{1,0:T(8,128)(2,1)S(1)}, bf16[1024,128]{1,0:T(8,128)(2,1)S(1)}, u32[]{:S(2)}, u32[]{:S(2)}) %collective-permute-start) | collective-permute-done | bytes 262176 | tf_op jit(solution)/shard_map/ppermute | solution.py:139
  105.7 3.1 collective-permute-start.1
  108.8 5.5 %collective-permute-done.1 = bf16[1024,128]{1,0:T(8,128)(2,1)S(1)} collective-permute-done((bf16[1024,128]{1,0:T(8,128)(2,1)S(1)}, bf16[1024,128]{1,0:T(8,128)(2,1)S(1)}, u32[]{:S(2)}, u32[]{:S(2)}) %collective-permute-start.1) | collective-permute-done | bytes 262176 | tf_op jit(solution)/shard_map/ppermute | solution.py:139
  114.4 3.4 collective-permute-start.2
  117.9 34.1 %all_gather.39 = bf16[1024,256]{1,0:T(8,128)(2,1)S(1)} all-gather(bf16[128,256]{1,0:T(8,128)(2,1)S(1)} %copy-done.7), channel_id=1, replica_groups=mesh['dp'=8,'mp'=4] {'dp'}, dimensions={0}, use_global_device_ids=true | all-gather | bytes 589824 | tf_op jit(solution)/shard_map/all_gather | solution.py:103
  152.1 3.3 collective-permute-start.3
  155.4 0.5 multiply_reduce_fusion
  155.8 5.8 %collective-permute-done.3 = bf16[1024,128]{1,0:T(8,128)(2,1)} collective-permute-done((bf16[1024,128]{1,0:T(8,128)(2,1)S(1)}, bf16[1024,128]{1,0:T(8,128)(2,1)}, u32[]{:S(2)}, u32[]{:S(2)}) %collective-permute-start.3) | collective-permute-done | bytes 262176 | tf_op jit(solution)/shard_map/ppermute | solution.py:139
  161.6 3.5 collective-permute-start.4
  165.5 5.5 %collective-permute-done.4 = bf16[1024,128]{1,0:T(8,128)(2,1)} collective-permute-done((bf16[1024,128]{1,0:T(8,128)(2,1)}, bf16[1024,128]{1,0:T(8,128)(2,1)}, u32[]{:S(2)}, u32[]{:S(2)}) %collective-permute-start.4) | collective-permute-done | bytes 262176 | tf_op jit(solution)/shard_map/ppermute | solution.py:139
  171.0 2.2 collective-permute-start.5
  173.2 34.3 %all_gather.38 = bf16[1024,256]{1,0:T(8,128)(2,1)S(1)} all-gather(bf16[128,256]{1,0:T(8,128)(2,1)} %param.31), channel_id=1, replica_groups=mesh['dp'=8,'mp'=4] {'dp'}, dimensions={0}, use_global_device_ids=true | all-gather | bytes 589824 | tf_op jit(solution)/shard_map/all_gather | solution.py:102
  207.5 0.3 convolution_convert_fusion.3
  207.8 1.3 collective-permute-start.6
  209.1 0.3 convolution_convert_fusion.4
  209.4 0.7 reshape.120
  210.1 0.6 dynamic-slice.6
  211.5 4.0 %collective-permute-done.6 = bf16[1024,128]{1,0:T(8,128)(2,1)S(1)} collective-permute-done((bf16[1024,128]{1,0:T(8,128)(2,1)S(1)}, bf16[1024,128]{1,0:T(8,128)(2,1)S(1)}, u32[]{:S(2)}, u32[]{:S(2)}) %collective-permute-start.6) | collective-permute-done | bytes 262176 | tf_op jit(solution)/shard_map/ppermute | solution.py:139
  215.5 0.7 constant_dynamic-update-slice_fusion.15
  216.2 0.7 constant_dynamic-update-slice_fusion.14
  216.9 1.7 constant_dynamic-update-slice_fusion.13
  218.7 1.7 constant_dynamic-update-slice_fusion.12
  220.4 0.8 constant_dynamic-update-slice_fusion.11
  221.1 0.7 constant_dynamic-update-slice_fusion.10
  221.9 0.7 constant_dynamic-update-slice_fusion.9
  222.6 0.7 constant_dynamic-update-slice_fusion.8
  223.3 1.6 fusion.15
  225.1 0.7 constant_dynamic-update-slice_fusion.7
  225.8 0.8 constant_dynamic-update-slice_fusion.6
  226.6 1.7 constant_dynamic-update-slice_fusion.5
  228.3 1.7 constant_dynamic-update-slice_fusion.4
  230.0 0.7 constant_dynamic-update-slice_fusion.3
  230.7 0.8 constant_dynamic-update-slice_fusion.2
  231.5 0.8 constant_dynamic-update-slice_fusion.1
  232.2 0.2 fusion.52
  232.5 2.5 fusion.51
  235.0 2.1 fusion.16
  237.1 0.3 fusion.14
  237.5 1.6 convolution_convert_fusion.2
  239.1 9.4 %fusion = bf16[56,1024]{1,0:T(8,128)(2,1)S(1)} fusion(bf16[200,1024]{1,0:T(8,128)(2,1)S(1)} %convolution_convert_fusion.2), kind=kCustom, calls=%all-reduce-scatter | all-reduce-scatter fusion | flops 229377 | bytes 524800
  248.5 1.9 collective-permute-start.7
  250.4 0.8 constant_dynamic-update-slice_fusion
  251.2 2.7 collective-permute-done.7
  254.4 6.3 %all-gather.2 = bf16[4,50,1024]{2,1,0:T(8,128)(2,1)S(1)} all-gather(bf16[1,50,1024]{2,1,0:T(8,128)(2,1)S(1)} %fusion.30), channel_id=1, replica_groups=mesh['dp'=8,'mp'=4] {'mp'}, dimensions={0}, use_global_device_ids=true | all-gather | bytes 512000 | tf_op jit(solution)/shard_map/all_gather | solution.py:151
  260.8 19.5 %all-gather.20.cloned.1.call-done = bf16[1024,1024]{1,0:T(8,128)(2,1)} async-done(((bf16[128,1024]{1,0:T(8,128)(2,1)}), bf16[1024,1024]{1,0:T(8,128)(2,1)}) %all-gather.20.cloned.1.call-update) | async-done | bytes 2097168 | tf_op jit(solution)/shard_map/all_gather | solution.py:133
  280.3 2.2 fusion.53
  282.5 47.6 %all-gather.22.cloned.1.call-done = bf16[1024,1024]{1,0:T(8,128)(2,1)} async-done(((bf16[128,1024]{1,0:T(8,128)(2,1)}), bf16[1024,1024]{1,0:T(8,128)(2,1)}) %all-gather.22.cloned.1.call-update) | async-done | bytes 2097168 | tf_op jit(solution)/shard_map/all_gather | solution.py:134
  330.1 3.3 fusion.8
  333.4 9.3 %fusion.1 = bf16[56,1024]{1,0:T(8,128)(2,1)S(1)} fusion(bf16[200,1024]{1,0:T(8,128)(2,1)S(1)} %fusion.8), kind=kCustom, calls=%all-reduce-scatter.1 | all-reduce-scatter fusion | flops 229377 | bytes 524800
  342.7 1.9 collective-permute-start.8
  344.7 3.5 collective-permute-done.8
  348.3 0.2 multiply_reduce_fusion.1
  348.6 2.2 fusion.40
  (72 shorter events, 2.1 us)
Async XLA Ops:
  7.2 148.2 %copy-start = (bf16[32,1024]{1,0:T(8,128)(2,1)S(1)}, bf16[32,1024]{1,0:T(8,128)(2,1)}, u32[]{:S(2)}) copy-start(bf16[32,1024]{1,0:T(8,128)(2,1)} %param.28) | copy-start | bytes 196612
  7.2 43.5 %copy-start.15 = (f32[2048]{0:T(1024)S(1)}, f32[2048]{0:T(1024)}, u32[]{:S(2)}) copy-start(f32[2048]{0:T(1024)} %param.25) | copy-start | bytes 24580
  7.2 43.5 %all-gather.14.cloned.1.call-start = ((), (), s32[]{:S(2)}) async-start(), calls=%async_computation.1 | async-start | bytes 1179648 | tf_op jit(solution)/shard_map/all_gather | solution.py:83
  7.9 83.9 %all-gather.16.cloned.1.call-start = ((), (), s32[]{:S(2)}) async-start(), calls=%async_computation.2 | async-start | bytes 1179648 | tf_op jit(solution)/shard_map/all_gather | solution.py:84
  8.7 214.7 %all-gather.12.cloned.1.call-start = ((), (), s32[]{:S(2)}) async-start(), calls=%async_computation | async-start | bytes 1179648 | tf_op jit(solution)/shard_map/all_gather | solution.py:101
  9.4 223.1 %all-gather.24.cloned.1.call-start = ((), (), s32[]{:S(2)}) async-start(), calls=%async_computation.6 | async-start | bytes 2621440 | tf_op jit(solution)/shard_map/all_gather | solution.py:119
  55.3 42.5 %copy-start.1 = (bf16[1024,128]{1,0:T(8,128)(2,1)S(1)}, bf16[1024,128]{1,0:T(8,128)(2,1)}, u32[]{:S(2)}) copy-start(bf16[1024,128]{1,0:T(8,128)(2,1)} %param.37) | copy-start | bytes 786436
  55.3 53.5 %copy-start.14 = (s32[4]{0:T(128)S(1)}, s32[4]{0:T(128)}, u32[]{:S(2)}) copy-start(s32[4]{0:T(128)} %param.24) | copy-start | bytes 52
  55.3 62.6 %copy-start.7 = (bf16[128,256]{1,0:T(8,128)(2,1)S(1)}, bf16[128,256]{1,0:T(8,128)(2,1)}, u32[]{:S(2)}) copy-start(bf16[128,256]{1,0:T(8,128)(2,1)} %param.32) | copy-start | bytes 196612
  55.4 100.0 %copy-start.5 = (f32[4,50,32]{1,2,0:T(8,128)S(1)}, f32[4,50,32]{1,2,0:T(8,128)}, u32[]{:S(2)}) copy-start(f32[4,50,32]{1,2,0:T(8,128)} %param.22) | copy-start | bytes 76804
  55.4 100.0 %copy-start.6 = (f32[4,50,32]{1,2,0:T(8,128)S(1)}, f32[4,50,32]{1,2,0:T(8,128)}, u32[]{:S(2)}) copy-start(f32[4,50,32]{1,2,0:T(8,128)} %param.23) | copy-start | bytes 76804
  55.4 179.6 %all-gather.26.cloned.1.call-start = ((), (), s32[]{:S(2)}) async-start(), calls=%async_computation.7 | async-start | bytes 2621440 | tf_op jit(solution)/shard_map/all_gather | solution.py:120
  96.4 68.9 %copy-start.9 = (f32[1024]{0:T(1024)S(1)}, f32[1024]{0:T(1024)}, u32[]{:S(2)}) copy-start(f32[1024]{0:T(1024)} %param.29) | copy-start | bytes 12292
  96.5 141.0 %all-gather.18.cloned.1.call-start = ((), (), s32[]{:S(2)}) async-start(), calls=%async_computation.3 | async-start | bytes 1179648 | tf_op jit(solution)/shard_map/all_gather | solution.py:131
  97.0 113.1 %copy-start.13 = (u32[32]{0:T(128)S(1)}, u32[32]{0:T(128)}, u32[]{:S(2)}) copy-start(u32[32]{0:T(128)} %constant.93) | copy-start | bytes 388
  97.0 114.3 %copy-start.12 = (s32[4]{0:T(128)S(1)}, s32[4]{0:T(128)}, u32[]{:S(2)}) copy-start(s32[4]{0:T(128)} %param.21) | copy-start | bytes 52
  97.1 183.2 %all-gather.20.cloned.1.call-start = ((), (), s32[]{:S(2)}) async-start(), calls=%async_computation.4 | async-start | bytes 2359296 | tf_op jit(solution)/shard_map/all_gather | solution.py:133
  97.8 232.3 %all-gather.22.cloned.1.call-start = ((), (), s32[]{:S(2)}) async-start(), calls=%async_computation.5 | async-start | bytes 2359296 | tf_op jit(solution)/shard_map/all_gather | solution.py:134
  97.9 7.8 %collective-permute-start = (bf16[1024,128]{1,0:T(8,128)(2,1)S(1)}, bf16[1024,128]{1,0:T(8,128)(2,1)S(1)}, u32[]{:S(2)}, u32[]{:S(2)}) collective-permute-start(bf16[1024,128]{1,0:T(8,128)(2,1)S(1)} %copy-done.1), channel_id=1, source_target_pairs={{0,4},{4,8},{8,12},{12,16},{16,20},{20,24},{24,28},{28,0},{1,5},{5... | collective-permute-start | bytes 786440 | tf_op jit(solution)/shard_map/ppermute | solution.py:139
  105.7 8.7 %collective-permute-start.1 = (bf16[1024,128]{1,0:T(8,128)(2,1)S(1)}, bf16[1024,128]{1,0:T(8,128)(2,1)S(1)}, u32[]{:S(2)}, u32[]{:S(2)}) collective-permute-start(bf16[1024,128]{1,0:T(8,128)(2,1)S(1)} %collective-permute-done), channel_id=1, source_target_pairs={{0,4},{4,8},{8,12},{12,16},{16,20},{20,24},{24,28},{28,0},{1,5},{5... | collective-permute-start | bytes 786440 | tf_op jit(solution)/shard_map/ppermute | solution.py:139
  114.4 37.7 %collective-permute-start.2 = (bf16[1024,128]{1,0:T(8,128)(2,1)S(1)}, bf16[1024,128]{1,0:T(8,128)(2,1)S(1)}, u32[]{:S(2)}, u32[]{:S(2)}) collective-permute-start(bf16[1024,128]{1,0:T(8,128)(2,1)S(1)} %collective-permute-done.1), channel_id=1, source_target_pairs={{0,4},{4,8},{8,12},{12,16},{16,20},{20,24},{24,28},{28,0},{1,5},{5... | collective-permute-start | bytes 786440 | tf_op jit(solution)/shard_map/ppermute | solution.py:139
  152.1 13.1 %copy-start.2 = (bf16[1024,128]{1,0:T(8,128)(2,1)}, bf16[1024,128]{1,0:T(8,128)(2,1)S(1)}, u32[]{:S(2)}) copy-start(bf16[1024,128]{1,0:T(8,128)(2,1)S(1)} %collective-permute-done.2) | copy-start | bytes 786436
  152.1 9.6 %collective-permute-start.3 = (bf16[1024,128]{1,0:T(8,128)(2,1)S(1)}, bf16[1024,128]{1,0:T(8,128)(2,1)}, u32[]{:S(2)}, u32[]{:S(2)}) collective-permute-start(bf16[1024,128]{1,0:T(8,128)(2,1)S(1)} %collective-permute-done.2), channel_id=1, source_target_pairs={{0,4},{4,8},{8,12},{12,16},{16,20},{20,24},{24,28},{28,0},{1,5},{5... | collective-permute-start | bytes 786440 | tf_op jit(solution)/shard_map/ppermute | solution.py:139
  161.6 9.4 %collective-permute-start.4 = (bf16[1024,128]{1,0:T(8,128)(2,1)}, bf16[1024,128]{1,0:T(8,128)(2,1)}, u32[]{:S(2)}, u32[]{:S(2)}) collective-permute-start(bf16[1024,128]{1,0:T(8,128)(2,1)} %collective-permute-done.3), channel_id=1, source_target_pairs={{0,4},{4,8},{8,12},{12,16},{16,20},{20,24},{24,28},{28,0},{1,5},{5... | collective-permute-start | bytes 786440 | tf_op jit(solution)/shard_map/ppermute | solution.py:139
  165.3 55.1 %copy-start.3 = (bf16[1024,128]{1,0:T(8,128)(2,1)S(1)}, bf16[1024,128]{1,0:T(8,128)(2,1)}, u32[]{:S(2)}) copy-start(bf16[1024,128]{1,0:T(8,128)(2,1)} %copy-done.2) | copy-start | bytes 786436
  171.0 36.8 %collective-permute-start.5 = (bf16[1024,128]{1,0:T(8,128)(2,1)}, bf16[1024,128]{1,0:T(8,128)(2,1)S(1)}, u32[]{:S(2)}, u32[]{:S(2)}) collective-permute-start(bf16[1024,128]{1,0:T(8,128)(2,1)} %collective-permute-done.4), channel_id=1, source_target_pairs={{0,4},{4,8},{8,12},{12,16},{16,20},{20,24},{24,28},{28,0},{1,5},{5... | collective-permute-start | bytes 786440 | tf_op jit(solution)/shard_map/ppermute | solution.py:139
  207.8 7.6 %collective-permute-start.6 = (bf16[1024,128]{1,0:T(8,128)(2,1)S(1)}, bf16[1024,128]{1,0:T(8,128)(2,1)S(1)}, u32[]{:S(2)}, u32[]{:S(2)}) collective-permute-start(bf16[1024,128]{1,0:T(8,128)(2,1)S(1)} %collective-permute-done.5), channel_id=1, source_target_pairs={{0,4},{4,8},{8,12},{12,16},{16,20},{20,24},{24,28},{28,0},{1,5},{5... | collective-permute-start | bytes 786440 | tf_op jit(solution)/shard_map/ppermute | solution.py:139
  231.5 5.6 %copy-start.4 = (bf16[4,50,256]{2,1,0:T(8,128)(2,1)S(1)}, bf16[4,50,256]{2,1,0:T(8,128)(2,1)}, u32[]{:S(2)}) copy-start(bf16[4,50,256]{2,1,0:T(8,128)(2,1)} %reshape.120) | copy-start | bytes 307204
  235.0 19.3 %copy-start.10 = (f32[1024]{0:T(1024)S(1)}, f32[1024]{0:T(1024)}, u32[]{:S(2)}) copy-start(f32[1024]{0:T(1024)} %param.34) | copy-start | bytes 12292
  248.5 5.4 %collective-permute-start.7 = (bf16[18,1024]{1,0:T(8,128)(2,1)S(1)}, bf16[18,1024]{1,0:T(8,128)(2,1)S(1)}, u32[]{:S(2)}, u32[]{:S(2)}) collective-permute-start(bf16[18,1024]{1,0:T(8,128)(2,1)S(1)} %slice), channel_id=1, source_target_pairs={{0,1},{1,2},{2,3},{4,5},{5,6},{6,7},{8,9},{9,10},{10,11},{12,13},{... | collective-permute-start | bytes 110600
  282.5 66.1 %copy-start.8 = (bf16[1024,32]{0,1:T(8,128)(2,1)S(1)}, bf16[1024,32]{0,1:T(8,128)(2,1)}, u32[]{:S(2)}) copy-start(bf16[1024,32]{0,1:T(8,128)(2,1)} %param.39) | copy-start | bytes 196612
  282.5 66.1 %copy-start.11 = (f32[1024]{0:T(1024)S(1)}, f32[1024]{0:T(1024)}, u32[]{:S(2)}) copy-start(f32[1024]{0:T(1024)} %param.38) | copy-start | bytes 12292
  342.7 5.4 %collective-permute-start.8 = (bf16[18,1024]{1,0:T(8,128)(2,1)S(1)}, bf16[18,1024]{1,0:T(8,128)(2,1)S(1)}, u32[]{:S(2)}, u32[]{:S(2)}) collective-permute-start(bf16[18,1024]{1,0:T(8,128)(2,1)S(1)} %slice.1), channel_id=1, source_target_pairs={{0,1},{1,2},{2,3},{4,5},{5,6},{6,7},{8,9},{9,10},{10,11},{12,13},{... | collective-permute-start | bytes 110600
Sparse Core Ops, SparseCore 0:
  10.1 40.5 all-gather.13
  52.8 38.9 all-gather.15
  94.0 44.5 all-gather.11
  139.9 22.9 all-gather.23
  164.4 22.5 all-gather.25
  188.9 40.5 all-gather.17
  231.6 48.7 all-gather.19
  282.4 47.6 all-gather.21
